TPU v7x, 32 devices: a whole 2x2x4 slice. The times are simulated.
32 devices in a mesh: gx: 4 (over y, core), gy: 2 (over x), gz: 4 (over z).
Axes of the slice: x: 2, y: 2, z: 4, core: 2. Of those that a mesh axis runs over, the one named last changes fastest.
Arguments:
- positions: float32 [3, 4, 2, 4, 512], P(None, 'gx', 'gy', 'gz'), may hold values from 0 to 1
- velocities: float32 [3, 4, 2, 4, 512], P(None, 'gx', 'gy', 'gz'), may hold values from -6 to 6
- charges: float32 [4, 2, 4, 512], P('gx', 'gy', 'gz'), may hold values from -5 to 5
- cluster_atoms: int32 [4, 2, 4, 768], P('gx', 'gy', 'gz'), may hold values from 0 to 512, as said below
- pair_list: int32 [3, 4, 2, 4, 256], P(None, 'gx', 'gy', 'gz'), may hold values from 0 to 124, as said below
Outputs:
- new_positions: float32 [3, 4, 2, 4, 512], P(None, 'gx', 'gy', 'gz')
- new_velocities: float32 [3, 4, 2, 4, 512], P(None, 'gx', 'gy', 'gz')
- last_forces: float32 [3, 4, 2, 4, 512], P(None, 'gx', 'gy', 'gz')
Inputs may be any that keep to these rules, and one draw needn't show every extreme that they name: `cluster_atoms`: on every domain each atom index below 512 stands in exactly one slot; all other slots hold 512, meaning empty. `pair_list`: row 0 and row 1 lie in 0 to 5, row 2 in 0 to 124; on every domain each of the 125 shift indices appears in at least 2 listed pairs.
All inputs are finite; a program needn't handle non-finite values.
Results may differ from a plain program's by a relative error of at most 0.0001.
Values sent between devices are 32-bit elements; how exact they have to be, the bound alone decides.
A program may use at most 64 MiB of HBM per device.

v0:
```python
import functools

import jax
import jax.numpy as jnp
from jax import lax
from jax.experimental import pallas as pl
from jax.experimental.pallas import tpu as pltpu
from jax.sharding import PartitionSpec as P

CLUSTER = 128
STEPS = 2
TIME_STEP = 0.02
MESH = pl.DeviceIdType.MESH
AXES = ("gx", "gy", "gz")
VMEM = pl.BlockSpec(memory_space=pltpu.VMEM)
SMEM = pl.BlockSpec(memory_space=pltpu.SMEM)
UNROLL = 32


def split3(value):
    hi = value.astype(jnp.bfloat16)
    rest = value - hi.astype(jnp.float32)
    mid = rest.astype(jnp.bfloat16)
    lo = (rest - mid.astype(jnp.float32)).astype(jnp.bfloat16)
    return hi, mid, lo


class Zone:
    def __init__(self, sizes):
        self.sizes = sizes
        self.spans = tuple(min(5, n) for n in sizes)
        self.lows = tuple(-2 if n >= 5 else 0 for n in sizes)
        self.count = self.spans[0] * self.spans[1] * self.spans[2]
        own = tuple(-low for low in self.lows)
        self.paired = max(sizes) <= 4 and sizes[0] % 2 == 0
        self.plane = self.spans[1] * self.spans[2]
        self.own = (own[0] * self.spans[1] + own[1]) * self.spans[2] + own[2]

    def place(self, deltas):
        index = 0
        for delta, n, span in zip(deltas, self.sizes, self.spans):
            if n >= 5:
                here = delta + 2
            elif n in (1, 2, 4):
                here = (delta + 2 * n) & (n - 1)
            else:
                here = lax.rem(delta + 2 * n, n)
            index = index * span + here
        return index

    def peer(self, index, sign):
        parts = (
            index // (self.spans[1] * self.spans[2]),
            (index // self.spans[2]) % self.spans[1],
            index % self.spans[2],
        )
        out = []
        for axis, n, low, part in zip(AXES, self.sizes, self.lows, parts):
            out.append((lax.axis_index(axis) + sign * (part + low) + 2 * n) % n)
        return tuple(out)

    def turn(self):
        return 1 - 2 * (lax.axis_index(AXES[0]) % 2)

    def partner(self):
        return (lax.axis_index(AXES[0]) + self.turn(),) + tuple(
            lax.axis_index(axis) for axis in AXES[1:]
        )

    def seen_by_partner(self, index):
        return (index - self.turn() * self.plane + self.count) % self.count

    def alike(self, body):
        def step(k, carry):
            body((k // self.plane) * 2 * self.plane + k % self.plane)
            return carry

        lax.fori_loop(1, self.count // 2, step, 0)

    def others(self, body):
        def step(k, carry):
            body((self.own + 1 + k) % self.count)
            return carry

        lax.fori_loop(0, self.count - 1, step, 0)


def one_hot(atoms_ref, atom_count):
    slots = atoms_ref.shape[1]
    rows = lax.broadcasted_iota(jnp.int32, (atom_count, slots), 0)
    return jnp.where(rows == atoms_ref[...], 1.0, 0.0).astype(jnp.bfloat16)


def rows_where(count, index):
    rows = lax.broadcasted_iota(jnp.int32, (count, index.shape[1]), 0)
    return jnp.where(rows == index, 1.0, 0.0).astype(jnp.bfloat16)


def exact_dot(selector, values):
    return sum(
        jnp.dot(selector, piece, preferred_element_type=jnp.float32) for piece in split3(values)
    )


def side_by_side(ref):
    return jnp.concatenate([ref[c] for c in range(ref.shape[0])], axis=1)


def share(zone, src, dst_ref, send_sem, recv_sem):
    def copy(index):
        return pltpu.make_async_remote_copy(
            src_ref=src,
            dst_ref=dst_ref.at[index],
            send_sem=send_sem.at[index],
            recv_sem=recv_sem.at[index],
            device_id=zone.peer(index, -1),
            device_id_type=MESH,
        )

    if not zone.paired:
        zone.others(lambda index: copy(index).start())
        zone.others(lambda index: copy(index).wait())
        return

    def relay(index, block):
        place = zone.seen_by_partner(index)
        return pltpu.make_async_remote_copy(
            src_ref=block,
            dst_ref=dst_ref.at[place],
            send_sem=send_sem.at[(index + zone.plane) % zone.count],
            recv_sem=recv_sem.at[place],
            device_id=zone.partner(),
            device_id_type=MESH,
        )

    zone.alike(lambda index: copy(index).start())
    relay(zone.own, src).start()

    def pass_on(index):
        copy(index).wait_recv()
        relay(index, dst_ref.at[index]).start()

    zone.alike(pass_on)
    zone.alike(lambda index: copy(index).wait_send())

    def settle(k, carry):
        index = (k // zone.plane) * 2 * zone.plane + k % zone.plane
        relay(index, src).wait_send()
        arrived = pltpu.make_async_remote_copy(
            src_ref=src,
            dst_ref=dst_ref.at[index + zone.plane],
            send_sem=send_sem.at[index + zone.plane],
            recv_sem=recv_sem.at[index + zone.plane],
            device_id=zone.partner(),
            device_id_type=MESH,
        )
        arrived.wait_recv()
        return carry

    lax.fori_loop(0, zone.count // 2, settle, 0)


def gathered_force(zone, force_ref, land_ref, send_sem, recv_sem):
    def copy(index):
        return pltpu.make_async_remote_copy(
            src_ref=force_ref.at[index],
            dst_ref=land_ref.at[index],
            send_sem=send_sem.at[index],
            recv_sem=recv_sem.at[index],
            device_id=zone.peer(index, 1),
            device_id_type=MESH,
        )

    if not zone.paired:
        zone.others(lambda index: copy(index).start())
        zone.others(lambda index: copy(index).wait())

        def add(k, total):
            return total + land_ref[(zone.own + 1 + k) % zone.count]

        return lax.fori_loop(0, zone.count - 1, add, force_ref[zone.own])

    def handed(part):
        odd = (2 * part + 1) * zone.plane
        return pltpu.make_async_remote_copy(
            src_ref=force_ref.at[pl.ds(odd, zone.plane)],
            dst_ref=land_ref.at[pl.ds(zone.count + zone.seen_by_partner(odd), zone.plane)],
            send_sem=send_sem.at[odd],
            recv_sem=recv_sem.at[zone.count + zone.seen_by_partner(odd)],
            device_id=zone.partner(),
            device_id_type=MESH,
        )

    def taken(part):
        even = 2 * part * zone.plane
        return pltpu.make_async_remote_copy(
            src_ref=force_ref.at[pl.ds(even, zone.plane)],
            dst_ref=land_ref.at[pl.ds(zone.count + even, zone.plane)],
            send_sem=send_sem.at[even],
            recv_sem=recv_sem.at[zone.count + even],
            device_id=zone.partner(),
            device_id_type=MESH,
        )

    parts = zone.count // (2 * zone.plane)
    for part in range(parts):
        handed(part).start()
    for part in range(parts):
        taken(part).wait_recv()
        even = 2 * part * zone.plane
        for k in range(zone.plane):
            force_ref[even + k] += land_ref[zone.count + even + k]
    zone.alike(lambda index: copy(index).start())
    for part in range(parts):
        handed(part).wait_send()
    zone.alike(lambda index: copy(index).wait())

    def add(k, total):
        return total + land_ref[(k // zone.plane) * 2 * zone.plane + k % zone.plane]

    return lax.fori_loop(1, zone.count // 2, add, force_ref[zone.own])


def weighted(coords, charge):
    charge = 0.125 * charge
    part = jnp.concatenate([charge * c for c in coords] + [charge], axis=0)
    pieces = [p.astype(jnp.float32) for p in split3(part)]
    stacked = jnp.concatenate(pieces + [jnp.zeros_like(part)], axis=0).astype(jnp.bfloat16)
    return jnp.concatenate([stacked, stacked], axis=1)


def folded(out):
    return out[0:4] + out[4:8] + out[8:12]


def shift_of(t):
    t25 = (t * 5243) >> 17
    t5 = (t * 205) >> 10
    return t25 - 2, t5 - 5 * t25 - 2, t - 5 * t5 - 2


def pair_forces(zone, clusters, pairs_ref, x_ref, q_ref, force_ref, left_ref, lw_ref,
                f_ref, right_sum_ref, left_sum_ref, zone_hot_ref, home_hot_ref):
    own = zone.own
    for k in range(clusters):
        coords = []
        for c in range(3):
            row = x_ref[own, pl.ds(c * clusters + k, 1), :]
            coords.append(row)
            left_ref[k, c] = jnp.transpose(jnp.broadcast_to(0.5 * row, (CLUSTER, CLUSTER)))
        lw_ref[k] = weighted(coords, q_ref[own, pl.ds(3 * clusters + k, 1), :])

    def right_side(p):
        j = pairs_ref[1, 0, p]
        deltas = shift_of(pairs_ref[2, 0, p])
        z = zone.place(deltas)
        coords = [
            x_ref[z, pl.ds(c * clusters + j, 1), :] + deltas[c].astype(jnp.float32)
            for c in range(3)
        ]
        return coords, q_ref[z, pl.ds(3 * clusters + j, 1), :]

    def geometry(b, which=range(UNROLL)):
        for n in which:
            p = b * UNROLL + n
            coords, _ = right_side(p)
            i = pairs_ref[0, 0, p]
            r2 = None
            for c in range(3):
                d = left_ref[i, c] - 0.5 * coords[c]
                r2 = d * d if r2 is None else r2 + d * d
            g = jnp.maximum(1.0 - r2, 0.0)
            den = r2 + 0.125
            start = pl.reciprocal(den, approx=True)
            t = (g * start) * (2.0 - den * start)
            f = (g * t) * (t + 3.0)
            hi = f.astype(jnp.bfloat16)
            f_ref[n, 0] = hi
            f_ref[n, 1] = (f - hi.astype(jnp.float32)).astype(jnp.bfloat16)

    def sums(b, which=range(UNROLL)):
        found = []
        for n in which:
            p = b * UNROLL + n
            hi, lo = f_ref[n, 0], f_ref[n, 1]
            coords, charge = right_side(p)
            left = lax.dot_general(
                weighted(coords, charge), jnp.concatenate([hi, lo], axis=1),
                (((1,), (1,)), ((), ())), preferred_element_type=jnp.float32,
            )
            right = jnp.dot(
                lw_ref[pairs_ref[0, 0, p]], jnp.concatenate([hi, lo], axis=0),
                preferred_element_type=jnp.float32,
            )
            found.append((p, coords, charge, left, right))
        return found

    def keep(found):
        for p, coords, charge, left, right in found:
            left = folded(left)
            right = folded(right)
            for c in range(4):
                left_sum_ref[c, pl.ds(p, 1), :] = left[c : c + 1]
            for c in range(3):
                right_sum_ref[c, pl.ds(p, 1), :] = charge * (
                    coords[c] * right[3:4] - right[c : c + 1]
                )

    blocks = pairs_ref.shape[2] // UNROLL
    geometry(0)

    def block(b, carry):
        found = []
        for n in range(UNROLL):
            found += sums(b - 1, [n])
            geometry(b, [n])
            if n > 1:
                keep(found[n - 2 : n - 1])
        keep(found[-2:])
        return carry

    lax.fori_loop(1, blocks, block, 0)
    keep(sums(blocks - 1))

    zone_out = exact_dot(zone_hot_ref[...], side_by_side(right_sum_ref))
    home_out = exact_dot(home_hot_ref[...], side_by_side(left_sum_ref))
    for z in range(zone.count):
        for c in range(3):
            force_ref[z, c * clusters : (c + 1) * clusters, :] = zone_out[
                z * 8 : z * 8 + clusters, c * CLUSTER : (c + 1) * CLUSTER
            ]
    for c in range(3):
        rows = slice(c * clusters, (c + 1) * clusters)
        total = home_out[0:clusters, 3 * CLUSTER :]
        moment = home_out[0:clusters, c * CLUSTER : (c + 1) * CLUSTER]
        charge = q_ref[own, 3 * clusters : 4 * clusters, :]
        force_ref[own, rows, :] += charge * (x_ref[own, rows, :] * total - moment)


def kernel(zone, pairs_ref, pairs_vec_ref, x_in, v_in, q_in, atoms_ref, x_out, v_out, f_out,
           zone0_ref, zone1_ref, vel_ref, pos_ref, force_ref, land_ref, slot_ref, left_ref, lw_ref, f_ref,
           right_sum_ref, left_sum_ref, zone_hot_ref, home_hot_ref, send_sem, recv_sem):
    atom_count = x_in.shape[2]
    slots = atoms_ref.shape[1]
    clusters = slots // CLUSTER
    rows = 3 * clusters
    own = zone.own
    barrier = pltpu.get_barrier_semaphore()
    zone.others(lambda index: pl.semaphore_signal(
        barrier, 1, device_id=zone.peer(index, 1), device_id_type=MESH))

    data = jnp.concatenate(
        [x_in[c] for c in range(3)] + [v_in[c] for c in range(3)]
        + [q_in[...], jnp.zeros((1, atom_count), jnp.float32)], axis=0
    )
    hi, mid, lo = split3(data)
    stacked = jnp.concatenate([hi, mid, lo, jnp.zeros_like(hi)], axis=0)
    out = jnp.dot(stacked, one_hot(atoms_ref, atom_count), preferred_element_type=jnp.float32)
    slot = out[0:8] + out[8:16] + out[16:24]
    for k in range(clusters):
        lanes = slice(k * CLUSTER, (k + 1) * CLUSTER)
        for c in range(3):
            zone0_ref[own, c * clusters + k, :] = slot[c, lanes]
            vel_ref[c * clusters + k, :] = slot[3 + c, lanes]
        zone0_ref[own, 3 * clusters + k, :] = slot[6, lanes]
    deltas = shift_of(pairs_vec_ref[2])
    zone_hot_ref[...] = rows_where(zone.count * 8, zone.place(deltas) * 8 + pairs_vec_ref[1])
    home_hot_ref[...] = rows_where(8, pairs_vec_ref[0])
    pl.semaphore_wait(barrier, zone.count - 1)
    share(zone, zone0_ref.at[own], zone0_ref, send_sem.at[0], recv_sem.at[0])

    for step in range(STEPS):
        x_ref = zone0_ref if step == 0 else zone1_ref.at[step - 1]
        pair_forces(zone, clusters, pairs_ref, x_ref, zone0_ref, force_ref, left_ref, lw_ref,
                    f_ref, right_sum_ref, left_sum_ref, zone_hot_ref, home_hot_ref)
        force = gathered_force(zone, force_ref, land_ref.at[step],
                               send_sem.at[2 * step + 1], recv_sem.at[2 * step + 1])
        velocity = vel_ref[...] + TIME_STEP * force
        coords = x_ref[own, 0:rows, :] + TIME_STEP * velocity
        if step < STEPS - 1:
            vel_ref[...] = velocity
            zone1_ref[step, own] = coords
            share(zone, zone1_ref.at[step, own], zone1_ref.at[step],
                  send_sem.at[2 * step + 2], recv_sem.at[2 * step + 2])

    slot_ref[...] = jnp.zeros_like(slot_ref)
    for k in range(clusters):
        lanes = slice(k * CLUSTER, (k + 1) * CLUSTER)
        for c in range(3):
            r = c * clusters + k
            slot_ref[pl.ds(c, 1), lanes] = coords[r : r + 1]
            slot_ref[pl.ds(3 + c, 1), lanes] = velocity[r : r + 1]
            slot_ref[pl.ds(6 + c, 1), lanes] = force[r : r + 1]
    stacked = jnp.concatenate(split3(slot_ref[...]), axis=0)
    out = lax.dot_general(
        stacked, one_hot(atoms_ref, atom_count), (((1,), (1,)), ((), ())),
        preferred_element_type=jnp.float32,
    )
    atom = out[0:16] + out[16:32] + out[32:48]
    for c in range(3):
        x_out[c] = atom[c : c + 1]
        v_out[c] = atom[3 + c : 4 + c]
        f_out[c] = atom[6 + c : 7 + c]


def shards(sizes, positions, velocities, charges, cluster_atoms, pair_list):
    zone = Zone(sizes)
    atom_count = positions.shape[-1]
    slots = cluster_atoms.shape[-1]
    pair_count = pair_list.shape[-1]
    clusters = slots // CLUSTER
    rows = 3 * clusters
    f32, bf16 = jnp.float32, jnp.bfloat16
    x = positions.reshape(3, 1, atom_count)
    v = velocities.reshape(3, 1, atom_count)
    q = charges.reshape(1, atom_count)
    atoms = cluster_atoms.reshape(1, slots)
    pairs = pair_list.reshape(3, 1, pair_count)
    shape = jax.ShapeDtypeStruct((3, 1, atom_count), f32)
    outs = pl.pallas_call(
        functools.partial(kernel, zone),
        out_shape=(shape, shape, shape),
        in_specs=[SMEM] + [VMEM] * 5,
        out_specs=(VMEM, VMEM, VMEM),
        scratch_shapes=[
            pltpu.VMEM((zone.count, 4 * clusters, CLUSTER), f32),
            pltpu.VMEM((STEPS - 1, zone.count, rows, CLUSTER), f32),
            pltpu.VMEM((rows, CLUSTER), f32),
            pltpu.VMEM((rows, CLUSTER), f32),
            pltpu.VMEM((zone.count, rows, CLUSTER), f32),
            pltpu.VMEM((STEPS, 2 * zone.count, rows, CLUSTER), f32),
            pltpu.VMEM((16, slots), f32),
            pltpu.VMEM((clusters, 3, CLUSTER, CLUSTER), f32),
            pltpu.VMEM((clusters, 16, 2 * CLUSTER), bf16),
            pltpu.VMEM((UNROLL, 2, CLUSTER, CLUSTER), bf16),
            pltpu.VMEM((3, pair_count, CLUSTER), f32),
            pltpu.VMEM((4, pair_count, CLUSTER), f32),
            pltpu.VMEM((zone.count * 8, pair_count), bf16),
            pltpu.VMEM((8, pair_count), bf16),
            pltpu.SemaphoreType.DMA((2 * STEPS, 2 * zone.count)),
            pltpu.SemaphoreType.DMA((2 * STEPS, 2 * zone.count)),
        ],
        compiler_params=pltpu.CompilerParams(collective_id=0, has_side_effects=True),
        name="leapfrog",
    )(pairs, pairs, x, v, q, atoms)
    return tuple(out.reshape(positions.shape) for out in outs)


def solution(mesh):
    spec3 = P(None, "gx", "gy", "gz", None)
    spec1 = P("gx", "gy", "gz", None)
    sizes = tuple(mesh.shape[axis] for axis in AXES)
    return jax.shard_map(
        functools.partial(shards, sizes),
        mesh=mesh,
        in_specs=(spec3, spec3, spec1, spec1, spec3),
        out_specs=(spec3, spec3, spec3),
        check_vma=False,
    )
```

profile of v0, /device:TPU:0, one launch (start us, length us, event | category | flops | bytes accessed | tf_op | source)
XLA Modules:
  0.0 80.7 jit_solution(4855087168671695760)
XLA Ops:
  0.6 77.4 %leapfrog.1 = (f32[3,1,512]{2,1,0:T(1,128)}, f32[3,1,512]{2,1,0:T(1,128)}, f32[3,1,512]{2,1,0:T(1,128)}) custom-call(s32[3,1,256]{2,1,0:T(1,128)} %bitcast.14, s32[3,1,256]{2,1,0:T(1,128)} %bitcast.15, f32[3,1,512]{2,1,0:T(1,128)} %bitcast.19, f32[3,1,512]{2,1,0:T(1,128)} %bitcast.20, f32[1,512]{1,0:T(1,128)} %bitcast.22, s32[1,768]{1,0:T(1,128)} %bitcast.21), custom_call_target="tpu_custom_call" | custom-call | tf_op jit(solution)/shard_map/leapfrog/pallas_call | solution.py:420
  78.0 0.0 copy-start.2
  78.0 0.7 copy-done.2
  78.7 0.0 copy-start.1
  78.7 0.6 copy.14
  79.3 0.1 copy-done.1
  79.4 0.0 copy-start
  79.4 0.6 copy.15
  80.0 0.1 copy-done
  80.1 0.6 copy.16
Async XLA Ops:
  78.0 0.7 copy-start.2
  78.7 0.7 copy-start.1
  79.4 0.7 copy-start
where the time goes:
time: 81 us; the launch traced here: 80.7 us
  Pallas kernels  77.4 us (96%)
  local copies, waits for them, and re-layouts  2.67 us (3%)
    pallas_call x1, Pallas kernels, shards(): pl.pallas_call(functools.partial(kernel, zone), out_shape=(shape, shape,...  77.4 us
    unnamed x9, local copies, waits for them, and re-layouts  2.67 us

commit v1 on v0

v1 whole, which is shorter than its diff:
```python
import functools

import jax
import jax.numpy as jnp
from jax import lax
from jax.experimental import pallas as pl
from jax.experimental.pallas import tpu as pltpu
from jax.sharding import PartitionSpec as P

CLUSTER = 128
STEPS = 2
TIME_STEP = 0.02
REACH = 2
SHIFTS = (2 * REACH + 1) ** 3
MESH = pl.DeviceIdType.MESH
AXES = ("gx", "gy", "gz")
VMEM = pl.BlockSpec(memory_space=pltpu.VMEM)
RING = 4
HAND_BLOCKS = 18


def split3(value):
    hi = value.astype(jnp.bfloat16)
    rest = value - hi.astype(jnp.float32)
    mid = rest.astype(jnp.bfloat16)
    lo = (rest - mid.astype(jnp.float32)).astype(jnp.bfloat16)
    return hi, mid, lo


def rounded(value):
    return value.astype(jnp.bfloat16).astype(jnp.float32)


class Zone:
    def __init__(self, sizes):
        self.sizes = sizes
        self.spans = tuple(min(2 * REACH + 1, n) for n in sizes)
        self.lows = tuple(-REACH if n > 2 * REACH else 0 for n in sizes)
        self.count = self.spans[0] * self.spans[1] * self.spans[2]
        self.paired = max(sizes) <= 2 * REACH and sizes[0] % 2 == 0
        self.own = 0
        for low, span in zip(self.lows, self.spans):
            self.own = self.own * span - low
        self.pairs = {z: 0 for z in range(self.count)}
        for t in range(SHIFTS):
            self.pairs[self.place(shift_of(t), 1)] += 2

    def place(self, deltas, turn):
        index = 0
        for axis, (delta, n, span) in enumerate(zip(deltas, self.sizes, self.spans)):
            if axis == 0:
                delta = delta * turn
            if n > 2 * REACH:
                here = delta + REACH
            elif n in (1, 2, 4):
                here = (delta + 2 * n) & (n - 1)
            else:
                here = (delta + 2 * n) % n if isinstance(delta, int) else lax.rem(delta + 2 * n, n)
            index = index * span + here
        return index

    def parts(self, index):
        return (
            index // (self.spans[1] * self.spans[2]),
            (index // self.spans[2]) % self.spans[1],
            index % self.spans[2],
        )

    def odd(self, index):
        return self.paired and self.parts(index)[0] % 2 == 1

    def seen_by_partner(self, index):
        dx, dy, dz = self.parts(index)
        return (((1 - dx) % self.sizes[0]) * self.spans[1] + dy) * self.spans[2] + dz

    def hops(self, index):
        if self.odd(index):
            index = self.seen_by_partner(index)
        near = []
        for n, low, part in zip(self.sizes, self.lows, self.parts(index)):
            off = (part + low) % n
            near.append(min(off, n - off))
        return (near[0] + 1) // 2 + near[1] + near[2]

    def turn(self):
        return 1 - 2 * (lax.axis_index(AXES[0]) % 2) if self.paired else 1

    def peer(self, index, signs):
        out = []
        for axis, n, low, part, sign in zip(AXES, self.sizes, self.lows, self.parts(index), signs):
            out.append((lax.axis_index(axis) + sign * (part + low) + 2 * n) % n)
        return tuple(out)

    def at(self, index):
        return self.peer(index, (self.turn(), 1, 1))

    def sees(self, index):
        turn = self.turn()
        return self.peer(index, (turn if self.odd(index) else -turn, -1, -1))

    def partner(self):
        return (lax.axis_index(AXES[0]) + self.turn(),) + tuple(
            lax.axis_index(axis) for axis in AXES[1:]
        )


class Plan:
    def __init__(self, zone, pair_count):
        extra = pair_count - 2 * SHIFTS
        others = sorted((z for z in range(zone.count) if z != zone.own), key=lambda z: (zone.hops(z), z))
        even = [z for z in others if not zone.odd(z)]
        beside = [z for z in others if zone.odd(z) and zone.hops(z) == 0]
        near = [z for z in even if zone.hops(z) == 1]
        mid = [z for z in even if zone.hops(z) == 2]
        far = [z for z in even if zone.hops(z) > 2]
        twins = lambda zones: [zone.seen_by_partner(z) for z in zones]
        if zone.paired:
            batches = [[zone.own], beside, mid, twins(mid), twins(far), far, twins(near), near]
        else:
            batches = [[zone.own], mid, far, near]
        self.batches = [batch for batch in batches if batch]
        self.order = [z for batch in self.batches for z in batch]
        self.rank = {z: n for n, z in enumerate(self.order)}
        self.first = [self.rank[batch[0]] for batch in self.batches]
        self.size = [len(batch) for batch in self.batches]
        self.second = [zone.odd(batch[0]) and batch != beside for batch in self.batches]
        self.twin = {}
        for n, batch in enumerate(self.batches):
            if self.second[n]:
                m = self.batches.index(twins(batch))
                self.twin[n], self.twin[m] = m, n
        self.direct = [n for n in range(1, len(self.batches)) if not self.second[n]]
        self.starts, self.ends, at = {}, {}, 0
        for z in self.order:
            self.starts[z] = at
            at += zone.pairs[z]
            self.ends[z] = at + extra


def shift_of(t):
    t25 = (t * 5243) >> 17
    t5 = (t * 205) >> 10
    return t25 - 2, t5 - 5 * t25 - 2, t - 5 * t5 - 2


def one_hot(atoms_ref, atom_count):
    slots = atoms_ref.shape[1]
    rows = lax.broadcasted_iota(jnp.int32, (atom_count, slots), 0)
    return jnp.where(rows == atoms_ref[...], 1.0, 0.0).astype(jnp.bfloat16)


def in_work_order(zone, plan, pairs_ref):
    count = pairs_ref.shape[2]
    f32, bf16 = jnp.float32, jnp.bfloat16
    place = zone.place(shift_of(pairs_ref[2]), zone.turn())
    rank = jnp.zeros(place.shape, jnp.int32)
    for n, z in enumerate(plan.order):
        rank = jnp.where(place == z, n, rank)
    key = (rank * count + lax.broadcasted_iota(jnp.int32, place.shape, 1)).astype(f32)
    key_col = jnp.transpose(jnp.broadcast_to(key, (8, count)))[:, 0:1]
    slot = jnp.sum(jnp.where(key_col < key, 1.0, 0.0), axis=0, keepdims=True)
    places = lax.broadcasted_iota(jnp.int32, (count, count), 0).astype(f32)
    hot = jnp.where(places == slot, 1.0, 0.0).astype(bf16)
    rows = [pairs_ref[0], pairs_ref[1], rank, pairs_ref[2]]
    rows = jnp.concatenate([row.astype(f32) for row in rows] + [jnp.zeros((4, count), f32)], axis=0)
    out = lax.dot_general(
        rows.astype(bf16), hot, (((1,), (1,)), ((), ())), preferred_element_type=f32,
    )
    return out.astype(jnp.int32)


def kernel(zone, plan, pairs_ref, x_in, v_in, q_in, atoms_ref, x_out, v_out, f_out,
           first_ref, later_ref, force_ref, land_ref, hand_ref, vel_ref, slot_ref, table_ref,
           shift_ref, a_ref, w_ref, f_ref, push_ref, order_vec_ref, order_ref,
           send_sem, recv_sem, order_sem):
    f32, bf16 = jnp.float32, jnp.bfloat16
    atom_count = x_in.shape[2]
    pair_count = pairs_ref.shape[2]
    slots = atoms_ref.shape[1]
    clusters = slots // CLUSTER
    rows3 = 3 * clusters
    own = zone.own
    barrier = pltpu.get_barrier_semaphore()
    for z in plan.order[1:]:
        pl.semaphore_signal(barrier, 1, device_id=zone.at(z), device_id_type=MESH)

    tile = (8, CLUSTER)
    sub = lax.broadcasted_iota(jnp.int32, tile, 0)
    comp = sub & 3
    upper = sub < 4
    keep_q = jnp.where(comp == 3, 0.0, 1.0)

    def turned(value, by):
        return pltpu.roll(value, by, 0)

    def coords_ref(step):
        return first_ref if step == 0 else later_ref.at[step - 1]

    data = jnp.concatenate(
        [x_in[c] for c in range(3)] + [v_in[c] for c in range(3)]
        + [q_in[...], jnp.zeros((1, atom_count), f32)], axis=0
    )
    stacked = jnp.concatenate(list(split3(data)) + [jnp.zeros(data.shape, bf16)], axis=0)
    out = jnp.dot(stacked, one_hot(atoms_ref, atom_count), preferred_element_type=f32)
    slot = out[0:8] + out[8:16] + out[16:24]
    for k in range(clusters):
        lanes = slice(k * CLUSTER, (k + 1) * CLUSTER)
        for c in range(3):
            first_ref[0, c * clusters + k, :] = slot[c, lanes]
            vel_ref[c * clusters + k, :] = slot[3 + c, lanes]
        first_ref[0, rows3 + k, :] = slot[6, lanes]

    def some(ref, n):
        return ref.at[pl.ds(plan.first[n], plan.size[n])]

    def coords_copy(step, n, z):
        ref = coords_ref(step)
        return pltpu.make_async_remote_copy(
            src_ref=ref.at[0], dst_ref=ref.at[plan.rank[z]],
            send_sem=send_sem.at[2 * step, 0], recv_sem=recv_sem.at[2 * step, n],
            device_id=zone.sees(z), device_id_type=MESH,
        )

    def force_copy(step, n, z):
        return pltpu.make_async_remote_copy(
            src_ref=force_ref.at[step, plan.rank[z]], dst_ref=land_ref.at[step, plan.rank[z]],
            send_sem=send_sem.at[2 * step + 1, 0], recv_sem=recv_sem.at[2 * step + 1, n],
            device_id=zone.at(z), device_id_type=MESH,
        )

    def relay_copy(step, n):
        ref, twin = coords_ref(step), plan.twin[n]
        return pltpu.make_async_remote_copy(
            src_ref=some(ref, n), dst_ref=some(ref, twin),
            send_sem=send_sem.at[2 * step, 1], recv_sem=recv_sem.at[2 * step, twin],
            device_id=zone.partner(), device_id_type=MESH,
        )

    def hand_copy(step, n):
        return pltpu.make_async_remote_copy(
            src_ref=some(force_ref.at[step], n), dst_ref=some(hand_ref.at[step], plan.twin[n]),
            send_sem=send_sem.at[2 * step + 1, 1], recv_sem=recv_sem.at[2 * step + 1, n],
            device_id=zone.partner(), device_id_type=MESH,
        )

    def arrived(ref, sem):
        pltpu.make_async_copy(ref, ref, sem).wait()

    def send_coords(step):
        for n in plan.direct:
            for z in plan.batches[n]:
                coords_copy(step, n, z).start()

    pl.semaphore_wait(barrier, zone.count - 1)
    send_coords(0)

    order_vec_ref[...] = in_work_order(zone, plan, pairs_ref)
    to_scalars = pltpu.make_async_copy(order_vec_ref, order_ref, order_sem)
    to_scalars.start()

    axis_rows = [jnp.where(comp == c, 1.0, 0.0) for c in range(4)]
    for t in range(SHIFTS):
        shift = axis_rows[3]
        for c, delta in enumerate(shift_of(t)):
            if delta:
                shift = shift + float(delta) * axis_rows[c]
        shift_ref[t] = shift

    def receive(step, n, got):
        if n == 0 or n in got:
            return
        got.add(n)
        if plan.second[n]:
            receive(step, plan.twin[n], got)
        arrived(some(coords_ref(step), n), recv_sem.at[2 * step, n])
        if n in plan.twin and not plan.second[n]:
            relay_copy(step, n).start()

    def arrive(step, n, got):
        receive(step, n, got)
        if 2 <= n < len(plan.batches) - 1 and plan.second[n + 1]:
            receive(step, plan.twin[n + 1], got)
        ref = coords_ref(step)
        for r in range(plan.first[n], plan.first[n] + plan.size[n]):
            for k in range(clusters):
                value = first_ref[r, pl.ds(rows3 + k, 1), :]
                for c in range(3):
                    value = jnp.where(comp == c, ref[r, pl.ds(c * clusters + k, 1), :], value)
                table_ref[r * clusters + k] = value

    def weights(value):
        return jnp.where(upper, value, value - rounded(value))

    def own_side(i):
        both = table_ref[i]
        charge = 0.125 * table_ref[i, pl.ds(3, 1), :]
        w_ref[i] = weights(charge * jnp.where(comp == 3, 1.0, both))
        half = 0.5 * both
        high = rounded(half)
        square = half * half
        rest = 1.0 - (square[0:1] + square[1:2] + square[2:3])
        first = rounded(rest)
        second = rounded(rest - first)
        third = rest - first - second
        top = jnp.where(comp == 3, 1.0, high)
        bottom = jnp.where(sub < 3, half - high, 0.0)
        bottom = jnp.where(sub == 3, 1.0, bottom)
        bottom = jnp.where(sub == 4, first, bottom)
        bottom = jnp.where(sub == 5, second, bottom)
        bottom = jnp.where(sub == 6, third, bottom)
        return jnp.concatenate([top, bottom], axis=0)

    def within(value, count):
        return jnp.minimum(jnp.maximum(value, 0), count - 1)

    def prepare(b):
        sides, lefts, dots = [], [], []
        for p in (2 * b, 2 * b + 1):
            i = within(order_ref[0, p], clusters)
            j = within(order_ref[2, p] * clusters + order_ref[1, p], zone.count * clusters)
            t = within(order_ref[3, p], SHIFTS)
            both = table_ref[j]
            charge = table_ref[j, pl.ds(3, 1), :]
            coords = both * keep_q + shift_ref[t]
            w = coords * charge
            sides.append((p, i, j, charge, w))
            lefts.append(weights(0.125 * w))
            square = coords * coords
            norm = -0.25 * (turned(square, 1) + turned(square, 2) + turned(square, 3))
            value = jnp.where(comp == 3, norm, coords)
            rest = value - rounded(value)
            top = jnp.where(upper, value, rest)
            bottom = jnp.where(sub < 3, value, jnp.where(sub == 3, rest - rounded(rest), 1.0))
            right = jnp.concatenate([top, bottom], axis=0).astype(bf16)
            dots.append(jnp.dot(a_ref[i], right, preferred_element_type=f32))
        left = jnp.concatenate(lefts, axis=0).astype(bf16)
        return sides, left, dots

    def geometry(b, state):
        for n, s in enumerate(state[2]):
            g = jnp.maximum(s, 0.0)
            t = g * pl.reciprocal(1.125 - g, approx=True)
            f = (g * t) * (t + 3.0)
            hi = f.astype(bf16)
            f_ref[b % RING, n, 0] = hi
            f_ref[b % RING, n, 1] = (f - hi.astype(f32)).astype(bf16)

    def sums(b, state):
        sides, left, _ = state
        (hi0, lo0), (hi1, lo1) = [[f_ref[b % RING, n, h] for h in range(2)] for n in range(2)]
        own_rows = jnp.concatenate([w_ref[sides[0][1]], w_ref[sides[1][1]]], axis=0).astype(bf16)
        right_out = jnp.dot(
            jnp.concatenate([own_rows, own_rows], axis=1),
            jnp.concatenate(
                [jnp.concatenate([hi0, hi1], axis=1), jnp.concatenate([lo0, lo1], axis=1)], axis=0
            ),
            preferred_element_type=f32,
        )
        left_out = lax.dot_general(
            jnp.concatenate([left, left], axis=1),
            jnp.concatenate(
                [jnp.concatenate([hi0, lo0], axis=1), jnp.concatenate([hi1, lo1], axis=1)], axis=0
            ),
            (((1,), (1,)), ((), ())), preferred_element_type=f32,
        )
        return left_out, right_out

    def picked(total, mask, read):
        return [acc + jnp.where(mask, read(c), 0.0) for c, acc in enumerate(total)]

    def kept(b, state, outs, home, away):
        left_out, right_out = outs
        for n, (p, i, j, charge, w) in enumerate(state[0]):
            rows = slice(8 * n, 8 * n + 8)
            lanes = slice(n * CLUSTER, (n + 1) * CLUSTER)
            left = left_out[rows, lanes]
            right = right_out[rows, lanes]
            right = right + turned(right, 4)
            push_ref[b % RING, n, 0] = left + turned(left, 4)
            push_ref[b % RING, n, 1] = w * right[3:4] - charge * right

            def read(side, c):
                return push_ref[b % RING, n, side, pl.ds(c, 1), :]

            home = picked(home, sub == i, functools.partial(read, 0))
            for z in plan.order:
                if plan.starts[z] <= p < plan.ends[z]:
                    total = away.get(z, [jnp.zeros(tile, f32)] * 3)
                    away[z] = picked(total, sub == j - plan.rank[z] * clusters, functools.partial(read, 1))
        return home

    blocks = pair_count // 2
    batch_at = {}
    for n, batch in enumerate(plan.batches):
        batch_at.setdefault(plan.starts[batch[0]] // 2, []).append(n)
    last_of = {z: (plan.ends[z] - 1) // 2 for z in plan.order}
    done_at = [max(last_of[z] for z in batch) for batch in plan.batches]
    to_scalars.wait()

    for step in range(STEPS):
        states, outs = {}, {}
        home, away = [jnp.zeros(tile, f32)] * 4, {}
        pending, got = [], set()

        def send(n):
            for z in plan.batches[n]:
                force_copy(step, n, z).start()

        def settle(now):
            for n in list(pending):
                other = plan.twin[n]
                if now is None or now >= done_at[other] + HAND_BLOCKS:
                    arrived(some(hand_ref.at[step], n), recv_sem.at[2 * step + 1, other])
                    for r in range(plan.first[n], plan.first[n] + plan.size[n]):
                        force_ref[step, r] = force_ref[step, r] + hand_ref[step, r]
                    send(n)
                    pending.remove(n)

        def finished(n):
            if n and plan.second[n]:
                hand_copy(step, n).start()
            elif n in plan.twin:
                pending.append(n)
            elif n:
                send(n)

        for turn in range(blocks + 3):
            for n in batch_at.get(turn, []):
                arrive(step, n, got)
            if turn == 0:
                rows = [own_side(i) for i in range(clusters)]
                for i in range(clusters):
                    a_ref[i] = jnp.transpose(rows[i]).astype(bf16)
            if turn < blocks:
                states[turn] = prepare(turn)
            if 0 <= turn - 1 < blocks:
                geometry(turn - 1, states[turn - 1])
            if 0 <= turn - 2 < blocks:
                outs[turn - 2] = sums(turn - 2, states[turn - 2])
            if 0 <= turn - 3:
                now = turn - 3
                home = kept(now, states.pop(now), outs.pop(now), home, away)
                for z in plan.order:
                    if last_of[z] == now:
                        total = away.pop(z)
                        if z == own:
                            own_total = total
                            continue
                        for c in range(3):
                            rows = slice(c * clusters, (c + 1) * clusters)
                            force_ref[step, plan.rank[z], rows, :] = total[c][0:clusters]
                for n in range(len(plan.batches)):
                    if done_at[n] == now:
                        finished(n)
                settle(now)
        settle(None)

        ref = coords_ref(step)
        charge = first_ref[0, rows3 : rows3 + clusters, :]
        for c in range(3):
            rows = slice(c * clusters, (c + 1) * clusters)
            push = charge * (ref[0, rows, :] * home[3][0:clusters] - home[c][0:clusters])
            force_ref[step, 0, rows, :] = own_total[c][0:clusters] + push
        force = force_ref[step, 0]
        for n in plan.direct:
            arrived(some(land_ref.at[step], n), recv_sem.at[2 * step + 1, n])
            for r in range(plan.first[n], plan.first[n] + plan.size[n]):
                force = force + land_ref[step, r]
        velocity = vel_ref[...] + TIME_STEP * force
        coords = ref[0, 0:rows3, :] + TIME_STEP * velocity
        if step < STEPS - 1:
            vel_ref[...] = velocity
            later_ref[step, 0] = coords
            send_coords(step + 1)

    slot_ref[...] = jnp.zeros_like(slot_ref)
    for k in range(clusters):
        lanes = slice(k * CLUSTER, (k + 1) * CLUSTER)
        for c in range(3):
            r = c * clusters + k
            slot_ref[pl.ds(c, 1), lanes] = coords[r : r + 1]
            slot_ref[pl.ds(3 + c, 1), lanes] = velocity[r : r + 1]
            slot_ref[pl.ds(6 + c, 1), lanes] = force[r : r + 1]
    stacked = jnp.concatenate(split3(slot_ref[...]), axis=0)
    out = lax.dot_general(
        stacked, one_hot(atoms_ref, atom_count), (((1,), (1,)), ((), ())),
        preferred_element_type=f32,
    )
    atom = out[0:16] + out[16:32] + out[32:48]
    for c in range(3):
        x_out[c] = atom[c : c + 1]
        v_out[c] = atom[3 + c : 4 + c]
        f_out[c] = atom[6 + c : 7 + c]
    direct = sum(plan.size[n] for n in plan.direct)
    passed = sum(plan.size[n] for n in plan.twin if plan.second[n])
    for step in range(STEPS):
        for half, ref in enumerate((coords_ref(step), force_ref.at[step])):
            for way, count in enumerate((direct, passed)):
                if count:
                    arrived(ref.at[pl.ds(0, count)], send_sem.at[2 * step + half, way])


def shards(sizes, positions, velocities, charges, cluster_atoms, pair_list):
    zone = Zone(sizes)
    atom_count = positions.shape[-1]
    slots = cluster_atoms.shape[-1]
    pair_count = pair_list.shape[-1]
    clusters = slots // CLUSTER
    rows = 3 * clusters
    plan = Plan(zone, pair_count)
    f32, bf16, i32 = jnp.float32, jnp.bfloat16, jnp.int32
    x = positions.reshape(3, 1, atom_count)
    v = velocities.reshape(3, 1, atom_count)
    q = charges.reshape(1, atom_count)
    atoms = cluster_atoms.reshape(1, slots)
    pairs = pair_list.reshape(3, 1, pair_count)
    shape = jax.ShapeDtypeStruct((3, 1, atom_count), f32)
    block = (rows, CLUSTER)
    outs = pl.pallas_call(
        functools.partial(kernel, zone, plan),
        out_shape=(shape, shape, shape),
        in_specs=[VMEM] * 5,
        out_specs=(VMEM, VMEM, VMEM),
        scratch_shapes=[
            pltpu.VMEM((zone.count, 4 * clusters, CLUSTER), f32),
            pltpu.VMEM((STEPS - 1, zone.count) + block, f32),
            pltpu.VMEM((STEPS, zone.count) + block, f32),
            pltpu.VMEM((STEPS, zone.count) + block, f32),
            pltpu.VMEM((STEPS, zone.count) + block, f32),
            pltpu.VMEM(block, f32),
            pltpu.VMEM((16, slots), f32),
            pltpu.VMEM((zone.count * clusters, 8, CLUSTER), f32),
            pltpu.VMEM((SHIFTS, 8, CLUSTER), f32),
            pltpu.VMEM((clusters, CLUSTER, 16), bf16),
            pltpu.VMEM((clusters, 8, CLUSTER), f32),
            pltpu.VMEM((RING, 2, 2, CLUSTER, CLUSTER), bf16),
            pltpu.VMEM((RING, 2, 2, 8, CLUSTER), f32),
            pltpu.VMEM((8, pair_count), i32),
            pltpu.SMEM((8, pair_count), i32),
            pltpu.SemaphoreType.DMA((2 * STEPS, 2)),
            pltpu.SemaphoreType.DMA((2 * STEPS, len(plan.batches))),
            pltpu.SemaphoreType.DMA,
        ],
        compiler_params=pltpu.CompilerParams(collective_id=0, has_side_effects=True),
        name="leapfrog",
    )(pairs, x, v, q, atoms)
    return tuple(out.reshape(positions.shape) for out in outs)


def solution(mesh):
    spec3 = P(None, "gx", "gy", "gz", None)
    spec1 = P("gx", "gy", "gz", None)
    sizes = tuple(mesh.shape[axis] for axis in AXES)
    return jax.shard_map(
        functools.partial(shards, sizes),
        mesh=mesh,
        in_specs=(spec3, spec3, spec1, spec1, spec3),
        out_specs=(spec3, spec3, spec3),
        check_vma=False,
    )
```

time: 81 us -> 54.4 us (0.67)
  Pallas kernels: 77.4 us -> 50.7 us
    pallas_call x1, Pallas kernels: 77.4 us -> 50.7 us  [shards(): pl.pallas_call(functools.partial(kernel, zone, plan), out_shape=(shape, s...]
where the time goes in v1:
time: 54.4 us; the launch traced here: 54 us
  Pallas kernels  50.7 us (93%)
  local copies, waits for them, and re-layouts  2.67 us (5%)
  between operations  0.65 us (1%)
    pallas_call x1, Pallas kernels, shards(): pl.pallas_call(functools.partial(kernel, zone, plan), out_shape=(shape, s...  50.7 us
    unnamed x9, local copies, waits for them, and re-layouts  2.67 us

profile of v1, /device:TPU:0, one launch (start us, length us, event | category | flops | bytes accessed | tf_op | source)
XLA Modules:
  0.0 54.0 jit_solution(16974147599928259511)
XLA Ops:
  0.6 50.7 %leapfrog.1 = (f32[3,1,512]{2,1,0:T(1,128)}, f32[3,1,512]{2,1,0:T(1,128)}, f32[3,1,512]{2,1,0:T(1,128)}) custom-call(s32[3,1,256]{2,1,0:T(1,128)} %bitcast.19, f32[3,1,512]{2,1,0:T(1,128)} %bitcast.17, f32[3,1,512]{2,1,0:T(1,128)} %bitcast.18, f32[1,512]{1,0:T(1,128)} %bitcast.21, s32[1,768]{1,0:T(1,128)} %bitcast.20), custom_call_target="tpu_custom_call" | custom-call | tf_op jit(solution)/shard_map/leapfrog/pallas_call | solution.py:519
  51.4 0.0 copy-start.2
  51.4 0.7 %copy-done.2 = f32[3,1,512]{2,1,0:T(1,128)S(1)} copy-done((f32[3,1,512]{2,1,0:T(1,128)S(1)}, f32[3,1,512]{2,1,0:T(1,128)}, u32[]{:S(2)}) %copy-start.2) | copy-done | bytes 6168
  52.1 0.0 copy-start.1
  52.1 0.6 %copy.14 = f32[3,1,1,1,512]{4,3,2,1,0:T(1,128)} copy(f32[3,1,1,1,512]{4,3,2,1,0:T(1,128)S(1)} %bitcast.16) | data formatting | bytes 12288
  52.7 0.1 copy-done.1
  52.8 0.0 copy-start
  52.8 0.6 %copy.15 = f32[3,1,1,1,512]{4,3,2,1,0:T(1,128)} copy(f32[3,1,1,1,512]{4,3,2,1,0:T(1,128)S(1)} %bitcast.15) | data formatting | bytes 12288
  53.3 0.1 copy-done
  53.4 0.6 %copy.16 = f32[3,1,1,1,512]{4,3,2,1,0:T(1,128)} copy(f32[3,1,1,1,512]{4,3,2,1,0:T(1,128)S(1)} %bitcast.14) | data formatting | bytes 12288
Async XLA Ops:
  51.4 0.7 %copy-start.2 = (f32[3,1,512]{2,1,0:T(1,128)S(1)}, f32[3,1,512]{2,1,0:T(1,128)}, u32[]{:S(2)}) copy-start(f32[3,1,512]{2,1,0:T(1,128)} %get-tuple-element.6) | copy-start | bytes 18436
  52.1 0.7 %copy-start.1 = (f32[3,1,512]{2,1,0:T(1,128)S(1)}, f32[3,1,512]{2,1,0:T(1,128)}, u32[]{:S(2)}) copy-start(f32[3,1,512]{2,1,0:T(1,128)} %get-tuple-element.7) | copy-start | bytes 18436
  52.8 0.7 %copy-start = (f32[3,1,512]{2,1,0:T(1,128)S(1)}, f32[3,1,512]{2,1,0:T(1,128)}, u32[]{:S(2)}) copy-start(f32[3,1,512]{2,1,0:T(1,128)} %get-tuple-element.8) | copy-start | bytes 18436
